TPU v7x, 32 devices: a whole 2x2x4 slice. The times are simulated.
32 devices in a mesh: rep: 4 (over x, core), mx: 2 (over y), my: 4 (over z).
Axes of the slice: x: 2, y: 2, z: 4, core: 2. Of those that a mesh axis runs over, the one named last changes fastest.
Arguments:
- coefficients: bfloat16 [2, 384, 384, 384], P(None, 'mx', 'my'), may hold values from -7.5 to 7.5
- noise_field: bfloat16 [128, 2, 1536, 1536], P(('rep', 'mx'), None, 'my'), may hold values from -96 to 96
- mode_table: bfloat16 [384, 1536], replicated, may hold values from -0.3125 to 0.3125
Outputs:
- update: bfloat16 [2, 384, 384, 384], P(None, 'mx', 'my', 'rep')
All inputs are finite; a program needn't handle non-finite values.
Results may differ from a plain program's by a relative error of at most 0.008.
Values may be sent and summed in bfloat16 or wider, within the bound.
A program may use at most 384 MiB of HBM per device.

v0:
```python
import jax
import jax.numpy as jnp
from jax import lax
from jax.sharding import PartitionSpec as P

DAMPING = 0.25


def body(coefficients, noise_field, mode_table):
    rep_index = lax.axis_index("rep")
    col_index = lax.axis_index("my")
    rep_count = lax.axis_size("rep")
    row_count = lax.axis_size("mx")
    col_count = lax.axis_size("my")
    planes_dev = noise_field.shape[0]
    planes_rep = planes_dev * row_count
    planes_all = planes_rep * rep_count
    mode_count = mode_table.shape[0]
    point_count = mode_table.shape[1]
    slab_first = point_count // 2 - planes_all // 2
    row_block = mode_count // row_count
    col_block = mode_count // col_count
    point_block = point_count // col_count
    own_block = mode_count // rep_count
    slab_own = lax.dynamic_slice_in_dim(
        mode_table, slab_first + rep_index * planes_rep, planes_rep, 1
    )
    zmodes = jnp.einsum(
        "pabk,kz->zpba", coefficients, slab_own, preferred_element_type=jnp.float32
    ).astype(jnp.bfloat16)
    zmodes = zmodes.reshape(planes_rep, 2, col_block * row_block)
    spread = lax.all_to_all(zmodes, "mx", split_axis=0, concat_axis=2, tiled=True)
    grouped = spread.reshape(planes_dev, 2, row_count, col_block, row_block)
    tiled_table = mode_table.reshape(row_count, row_block, point_count)
    own_points = lax.dynamic_slice_in_dim(tiled_table, col_index * point_block, point_block, 2)
    block_part = jnp.einsum(
        "zpsal,slx->zpax",
        lax.all_gather(grouped, "my", axis=3, tiled=True),
        own_points,
        preferred_element_type=jnp.float32,
    ).astype(jnp.bfloat16)
    wave_field = jnp.einsum(
        "zpax,ay->zpxy", block_part, mode_table, preferred_element_type=jnp.float32
    )
    wave_real = wave_field[:, 0]
    wave_imag = wave_field[:, 1]
    density = wave_real * wave_real + wave_imag * wave_imag
    noise_wide = noise_field.astype(jnp.float32)
    drive_term = jnp.stack(
        [
            density * (wave_imag - DAMPING * wave_real) + noise_wide[:, 0],
            density * (-wave_real - DAMPING * wave_imag) + noise_wide[:, 1],
        ],
        1,
    ).astype(jnp.bfloat16)
    proj_columns = jnp.einsum(
        "zpxy,ny->zpnx", drive_term, mode_table, preferred_element_type=jnp.float32
    ).astype(jnp.bfloat16)
    block_part = lax.all_to_all(proj_columns, "my", split_axis=2, concat_axis=3, tiled=True)
    folded = jnp.einsum(
        "zpax,slx->zpsal", block_part, tiled_table, preferred_element_type=jnp.float32
    ).astype(jnp.bfloat16)
    proj_rows = folded.reshape(
        block_part.shape[0], block_part.shape[1], row_count * col_block * row_block
    )
    gathered_rows = lax.all_to_all(proj_rows, "mx", split_axis=2, concat_axis=0, tiled=True)
    slab_back = lax.dynamic_slice_in_dim(mode_table, rep_index * own_block, own_block, 0)[
        :, slab_first : slab_first + planes_all
    ]
    portion = lax.all_gather(gathered_rows, "rep", axis=0, tiled=True)
    plane_grid = portion.reshape(portion.shape[0], 2, col_block, row_block)
    summed = jnp.einsum("zpba,nz->pabn", plane_grid, slab_back, preferred_element_type=jnp.float32)
    return summed.astype(jnp.bfloat16)


def solution(mesh):
    in_specs = (P(None, "mx", "my", None), P(("rep", "mx"), None, "my", None), P())
    out_specs = P(None, "mx", "my", "rep")
    return jax.shard_map(body, mesh=mesh, in_specs=in_specs, out_specs=out_specs, check_vma=False)
```

profile of v0, /device:TPU:0, one launch (start us, length us, event | category | flops | bytes accessed | tf_op | source)
XLA Modules:
  0.0 974.5 jit_solution(4171945368356783076)
XLA Ops:
  7.8 25.5 %convert_bitcast_fusion.3 = bf16[32,2,96,192]{2,0,3,1:T(8,128)(2,1)} fusion(bf16[2,192,96,384]{3,2,1,0:T(8,128)(2,1)} %param.3, bf16[384,1536]{1,0:T(8,128)(2,1)S(1)} %copy-done, s32[]{:T(128)S(6)} %select_n.10), kind=kOutput, calls=%fused_computation.17 | convolution fusion | flops 907149312 | bytes 30769156 | tf_op jit(solution)/shard_map/pabk,kz->zpba/dot_general | solution.py:28
  33.3 5.1 copy.45
  38.5 6.9 reshape.28
  45.3 31.7 %all_to_all.51 = bf16[32,2,18432]{2,1,0:T(2,128)(2,1)S(1)} all-to-all(bf16[32,2,18432]{2,1,0:T(2,128)(2,1)S(1)} %reshape.28), channel_id=1, replica_groups=mesh['rep'=4,'mx'=2,'my'=4] {'mx'}, dimensions={0} | all-to-all | bytes 4718592 | tf_op jit(solution)/shard_map/all_to_all | solution.py:32
  84.3 38.0 %convert_element_type.34 = f32[16,2,384,1536]{3,2,1,0:T(8,128)} convert(bf16[16,2,384,1536]{3,2,1,0:T(8,128)(2,1)} %param.4) | non-fusion elementwise | flops 18874368 | bytes 113246208 | tf_op jit(solution)/shard_map/convert_element_type | solution.py:48
  122.3 180.6 %all-gather.3.cloned.1.call-done = bf16[16,2,2,384,192]{4,3,2,1,0:T(8,128)(2,1)} async-done(((bf16[16,2,2,96,192]{4,3,2,1,0:T(8,128)(2,1)}), bf16[16,2,2,384,192]{4,3,2,1,0:T(8,128)(2,1)}) %all-gather.3.cloned.1.call-update) | async-done | bytes 9437200 | tf_op jit(solution)/shard_map/all_gather | solution.py:38
  302.9 36.1 %fusion.6 = f32[16,2,384,1536]{3,2,1,0:T(8,128)} fusion(bf16[16,2,2,384,192]{4,3,2,1,0:T(8,128)(2,1)} %all-gather.3.cloned.1.call-done, bf16[384,1536]{1,0:T(8,128)(2,1)S(1)} %copy-done, bf16[2,192,1536]{2,1,0:T(8,128)(2,1)S(1)} %bitcast.69, s32[]{:T(128)S(6)} %select_n.11), kind=kOutput, calls=%fused_computation.10 | convolution fusion | flops 18124111872 | bytes 86409216 | tf_op jit(solution)/shard_map/zpax,ay->zpxy/dot_general | solution.py:42
  339.0 61.5 %fusion.1 = (bf16[16,1,384,1536]{3,2,1,0:T(8,128)(2,1)}, bf16[16,1,384,1536]{3,2,1,0:T(8,128)(2,1)}) fusion(f32[16,2,384,1536]{3,2,1,0:T(8,128)} %convert_element_type.34, f32[16,2,384,1536]{3,2,1,0:T(8,128)} %fusion.6), kind=kLoop, calls=%fused_computation.3 | loop fusion | flops 132120576 | bytes 188743680 | tf_op jit(solution)/shard_map/convert
  400.5 27.1 %convert_bitcast_fusion.1 = bf16[16,2,384,384]{2,3,1,0:T(8,128)(2,1)} fusion(bf16[16,1,384,1536]{3,2,1,0:T(8,128)(2,1)} %get-tuple-element.6, bf16[16,1,384,1536]{3,2,1,0:T(8,128)(2,1)} %get-tuple-element.5, bf16[384,1536]{1,0:T(8,128)(2,1)S(1)} %copy-done), kind=kOutput, calls=%fused_computation.15 | convolution fusion | flops 14519107584 | bytes 48365568 | tf_op jit(solution)/shard_map/zpxy,ny->zpnx/dot_general | solution.py:56
  427.5 23.9 %copy.29 = bf16[16,2,384,384]{3,1,0,2:T(2,128)(2,1)} copy(bf16[16,2,384,384]{2,3,1,0:T(8,128)(2,1)} %convert_bitcast_fusion.1) | data formatting | bytes 18874368 | tf_op jit(solution)/shard_map/convert_element_type | solution.py:58
  451.4 214.1 %all_to_all.52 = bf16[16,2,384,384]{3,1,0,2:T(2,128)(2,1)} all-to-all(bf16[16,2,384,384]{3,1,0,2:T(2,128)(2,1)} %copy.29), channel_id=1, replica_groups=mesh['rep'=4,'mx'=2,'my'=4] {'my'}, dimensions={2} | all-to-all | bytes 18874368 | tf_op jit(solution)/shard_map/all_to_all | solution.py:59
  665.5 10.9 %copy.30 = bf16[16,2,384,384]{3,2,1,0:T(8,128)(2,1)} copy(bf16[16,2,384,384]{3,1,0,2:T(2,128)(2,1)} %all_to_all.52) | data formatting | bytes 18874368 | tf_op jit(solution)/shard_map/all_to_all | solution.py:59
  676.4 10.6 %copy.31 = bf16[16,2,96,4,384]{4,3,2,1,0:T(4,128)(2,1)} copy(bf16[16,2,96,4,384]{4,2,3,1,0:T(8,128)(2,1)} %bitcast.73) | data formatting | bytes 18874368 | tf_op jit(solution)/shard_map/all_to_all | solution.py:59
  687.0 15.9 %reshape.25 = bf16[16,2,96,1536,1]{3,2,1,0,4:T(8,128)(2,1)} reshape(bf16[16,2,96,4,384]{4,3,2,1,0:T(4,128)(2,1)} %copy.31) | data formatting | bytes 18874368 | tf_op jit(solution)/shard_map/all_to_all | solution.py:59
  702.9 10.2 %convert_bitcast_fusion.2 = bf16[16,2,2,96,192]{4,3,2,1,0:T(8,128)(2,1)} fusion(bf16[2,192,1536,1,1]{2,1,0,4,3:T(8,128)(2,1)S(1)} %bitcast.68, bf16[16,2,96,1536,1]{3,2,1,0,4:T(8,128)(2,1)} %reshape.25), kind=kOutput, calls=%fused_computation.16 | convolution fusion | flops 3625058304 | bytes 12976128 | tf_op jit(solution)/shard_map/zpax,slx->zpsal/dot_general | solution.py:60
  713.1 35.2 %copy.46 = bf16[16,2,2,96,192]{0,1,4,3,2:T(2,128)(2,1)} copy(bf16[16,2,2,96,192]{4,3,2,1,0:T(8,128)(2,1)} %convert_bitcast_fusion.2) | data formatting | bytes 4718592 | tf_op jit(solution)/shard_map/reshape | solution.py:63
  748.3 27.0 %reshape.30 = bf16[2,2,294912]{2,1,0:T(2,128)(2,1)S(1)} reshape(bf16[36864,2,16]{2,1,0:T(2,128)(2,1)} %bitcast.70) | data formatting | bytes 4718592
  775.3 30.9 %all_to_all.53 = bf16[2,2,294912]{2,1,0:T(2,128)(2,1)} all-to-all(bf16[2,2,294912]{2,1,0:T(2,128)(2,1)S(1)} %reshape.30), channel_id=1, replica_groups=mesh['rep'=4,'mx'=2,'my'=4] {'mx'}, dimensions={0} | all-to-all | bytes 4718592 | tf_op jit(solution)/shard_map/all_to_all | solution.py:66
  806.2 22.4 %reshape.31 = bf16[36864,2,16]{2,1,0:T(2,128)(2,1)} reshape(bf16[2,2,294912]{2,1,0:T(2,128)(2,1)} %all_to_all.53) | data formatting | bytes 4718592
  828.6 35.6 %copy.34 = bf16[2,16,2,18432]{3,1,0,2:T(8,128)(2,1)} copy(bf16[2,16,2,18432]{1,2,3,0:T(2,128)(2,1)} %bitcast.71) | data formatting | bytes 4718592 | tf_op jit(solution)/shard_map/all_to_all | solution.py:66
  864.2 62.8 %all-gather.5.cloned.1.call-done = bf16[128,2,18432]{2,0,1:T(8,128)(2,1)} async-done(((bf16[32,2,18432]{2,0,1:T(8,128)(2,1)}), bf16[128,2,18432]{2,0,1:T(8,128)(2,1)}) %all-gather.5.cloned.1.call-update) | async-done | bytes 9437200 | tf_op jit(solution)/shard_map/all_gather | solution.py:70
  927.0 12.6 %copy.35 = bf16[128,2,18432]{0,2,1:T(8,128)(2,1)} copy(bf16[128,2,18432]{2,0,1:T(8,128)(2,1)} %all-gather.5.cloned.1.call-done) | data formatting | bytes 18874368 | tf_op jit(solution)/shard_map/all_gather | solution.py:70
  939.6 13.8 %convert_bitcast_fusion = bf16[2,192,96,96]{1,3,2,0:T(8,128)(2,1)} fusion(bf16[128,2,96,192]{0,3,2,1:T(8,128)(2,1)} %bitcast.72, bf16[384,1536]{1,0:T(8,128)(2,1)S(1)} %copy-done, s32[]{:T(128)S(6)} %select_n.9, s32[]{:T(128)S(6)} %add.30), kind=kOutput, calls=%fused_computation.14 | convolution fusion | flops 909508608 | bytes 16539656 | tf_op jit(solution)/shard_map/zpba,nz->pabn/dot_general | solution.py:72
  953.4 13.9 %copy.36 = bf16[2,192,96,96]{3,2,1,0:T(8,128)(2,1)} copy(bf16[2,192,96,96]{1,3,2,0:T(8,128)(2,1)} %convert_bitcast_fusion) | data formatting | bytes 14155776 | tf_op jit(solution)/shard_map/convert_element_type | solution.py:73
  (8 shorter events, 8.5 us)
Async XLA Ops:
  6.5 1.3 copy-start
  6.5 296.3 %all-gather.3.cloned.1.call-start = ((), (), s32[]{:S(2)}) async-start(), calls=%async_computation.3 | async-start | bytes 15728640 | tf_op jit(solution)/shard_map/all_gather | solution.py:38
  84.0 843.0 %all-gather.5.cloned.1.call-start = ((), (), s32[]{:S(2)}) async-start(), calls=%async_computation.4 | async-start | bytes 11796480 | tf_op jit(solution)/shard_map/all_gather | solution.py:70
Sparse Core Ops, SparseCore 0:
  84.1 218.6 all-gather.2
  864.4 62.5 all-gather.4
where the time goes:
time: 986 us; the launch traced here: 975 us
  blocking collectives  277 us (28%)
  waiting for transfers between devices  243 us (25%)
  local copies, waits for them, and re-layouts  228 us (23%)
  matrix products  113 us (11%)
  other arithmetic  99.5 us (10%)
  between operations  13.9 us (1%)
    all_to_all x1, blocking collectives, body(): lax.all_to_all(proj_columns, 'my', split_axis=2, concat_axis=3, tiled=True)  214 us
    all_gather x1, waiting for transfers between devices, body(): lax.all_gather(grouped, 'my', axis=3, tiled=True)  181 us
    all_gather x1, waiting for transfers between devices, body(): portion = lax.all_gather(gathered_rows, 'rep', axis=0, tiled=True)  62.8 us
    another operation x1, other arithmetic  61.5 us
    unnamed x4, local copies, waits for them, and re-layouts  50.7 us
    convert_element_type x1, other arithmetic, body(): noise_wide = noise_field.astype(jnp.float32)  38 us
    all_to_all x3, local copies, waits for them, and re-layouts, body(): lax.all_to_all(proj_columns, 'my', split_axis=2, concat_axis=3, tiled=True)  37.4 us
    dot_general x1, matrix products, body(): jnp.einsum('zpax,ay->zpxy', block_part, mode_table, preferred_element_typ...  36.1 us
  transfers between devices with their start and end apart: 2, of which 2 were waited for; matrix products, arithmetic and copies ran while one was open for 4% of the time, Pallas kernels for 0%

commit v1 on v0

--- a/solution.py
+++ b/solution.py
@@ -1,12 +1,16 @@
 import jax
 import jax.numpy as jnp
 from jax import lax
+from jax.experimental import pallas as pl
+from jax.experimental.pallas import tpu as pltpu
 from jax.sharding import PartitionSpec as P
 
 DAMPING = 0.25
-
-
-def body(coefficients, noise_field, mode_table):
+MESH = pl.DeviceIdType.MESH
+NT = (((1,), (1,)), ((), ()))
+
+
+def plain_body(coefficients, noise_field, mode_table):
     rep_index = lax.axis_index("rep")
     col_index = lax.axis_index("my")
     rep_count = lax.axis_size("rep")
@@ -72,6 +76,293 @@
     summed = jnp.einsum("zpba,nz->pabn", plane_grid, slab_back, preferred_element_type=jnp.float32)
     return summed.astype(jnp.bfloat16)
 
+def slab_kernel(own_ref, noise_ref, table_ref, turned_ref, out_ref, modes, parts, landed, noise,
+                own_sem, noise_sem, gather_recv, gather_send, sum_recv, sum_send):
+    count = lax.axis_size("my")
+    me = lax.axis_index("my")
+    planes = own_ref.shape[0]
+    block = own_ref.shape[2]
+    mode_count, point_count = table_ref.shape
+    chunk = max(c for c in (512, 256, 128) if point_count % c == 0)
+    up = {"my": me + 1}
+    down = {"my": me - 1}
+    has_up = me < count - 1
+    has_down = me > 0
+
+    barrier = pltpu.get_barrier_semaphore()
+
+    @pl.when(has_up)
+    def _():
+        pl.semaphore_signal(barrier, inc=1, device_id=up, device_id_type=MESH)
+
+    @pl.when(has_down)
+    def _():
+        pl.semaphore_signal(barrier, inc=1, device_id=down, device_id_type=MESH)
+
+    def rows(j):
+        return pl.ds(pl.multiple_of(j * block, block), block)
+
+    def own_copy():
+        return pltpu.make_async_copy(own_ref, modes.at[:, :, rows(me)], own_sem)
+
+    def noise_copy(p):
+        slot = lax.rem(p, 2)
+        return pltpu.make_async_copy(noise_ref.at[p], noise.at[slot], noise_sem.at[slot])
+
+    def gather_copy(p, j, way):
+        return pltpu.make_async_remote_copy(
+            src_ref=modes.at[p, :, rows(j)],
+            dst_ref=modes.at[p, :, rows(j)],
+            send_sem=gather_send.at[p, way, j],
+            recv_sem=gather_recv.at[p, j],
+            device_id=down if way else up,
+            device_id_type=MESH,
+        )
+
+    def sum_copy(p, j, way, slot):
+        return pltpu.make_async_remote_copy(
+            src_ref=parts.at[p, :, rows(j)],
+            dst_ref=landed.at[p, slot],
+            send_sem=sum_send.at[p, way, j],
+            recv_sem=sum_recv.at[p, slot],
+            device_id=down if way else up,
+            device_id_type=MESH,
+        )
+
+    own_copy().start()
+    noise_copy(0).start()
+    if planes > 1:
+        noise_copy(1).start()
+
+    pl.semaphore_wait(barrier, has_up.astype(jnp.int32) + has_down.astype(jnp.int32))
+
+    own_copy().wait()
+
+    def inside(p):
+        return jnp.logical_and(p >= 0, p < planes)
+
+    def step(s, carry):
+        @pl.when(s < planes)
+        def _():
+            @pl.when(has_up)
+            def _():
+                gather_copy(s, me, 0).start()
+
+            @pl.when(has_down)
+            def _():
+                gather_copy(s, me, 1).start()
+
+        for far in range(1, count):
+            p = s - far
+
+            @pl.when(jnp.logical_and(inside(p), me - far >= 0))
+            def _():
+                gather_copy(p, me - far, 0).wait_recv()
+
+                @pl.when(has_up)
+                def _():
+                    gather_copy(p, me - far, 0).start()
+
+            @pl.when(jnp.logical_and(inside(p), me + far <= count - 1))
+            def _():
+                gather_copy(p, me + far, 1).wait_recv()
+
+                @pl.when(has_down)
+                def _():
+                    gather_copy(p, me + far, 1).start()
+
+        c = s - (count - 1)
+
+        @pl.when(inside(c))
+        def _():
+            noise_copy(c).wait()
+            slot = lax.rem(c, 2)
+            turned = turned_ref[...]
+            lines = [
+                lax.dot_general(turned, modes[c, part], NT, preferred_element_type=jnp.float32)
+                .astype(jnp.bfloat16)
+                for part in range(2)
+            ]
+            columns = [None, None]
+            for first in range(0, point_count, chunk):
+                span = slice(first, first + chunk)
+                table = table_ref[:, span]
+                wave_real, wave_imag = [
+                    jnp.dot(line, table, preferred_element_type=jnp.float32) for line in lines
+                ]
+                density = wave_real * wave_real + wave_imag * wave_imag
+                noise_real = noise[slot, 0, :, span].astype(jnp.float32)
+                noise_imag = noise[slot, 1, :, span].astype(jnp.float32)
+                drive = [
+                    density * (wave_imag - DAMPING * wave_real) + noise_real,
+                    density * (-wave_real - DAMPING * wave_imag) + noise_imag,
+                ]
+                for part in range(2):
+                    more = lax.dot_general(
+                        table, drive[part].astype(jnp.bfloat16), NT,
+                        preferred_element_type=jnp.float32,
+                    )
+                    columns[part] = more if first == 0 else columns[part] + more
+            for part in range(2):
+                parts[c, part] = jnp.dot(
+                    columns[part].astype(jnp.bfloat16), turned, preferred_element_type=jnp.float32
+                ).astype(jnp.bfloat16)
+
+            @pl.when(c + 2 < planes)
+            def _():
+                noise_copy(c + 2).start()
+
+        def add(p, j, slot):
+            wide = parts[p, :, rows(j)].astype(jnp.float32) + landed[p, slot].astype(jnp.float32)
+            parts[p, :, rows(j)] = wide.astype(jnp.bfloat16)
+
+        rising = c - me
+        for far in range(count - 1, 0, -1):
+            @pl.when(jnp.logical_and(inside(rising), me + far <= count - 1))
+            def _():
+                j = me + far
+
+                @pl.when(has_down)
+                def _():
+                    sum_copy(rising, j, 0, j).wait_recv()
+                    add(rising, j, j)
+
+                sum_copy(rising, j, 0, j).start()
+
+        sinking = c - (count - 1 - me)
+        for far in range(count - 1, 0, -1):
+            @pl.when(jnp.logical_and(inside(sinking), me - far >= 0))
+            def _():
+                j = me - far
+
+                @pl.when(has_up)
+                def _():
+                    sum_copy(sinking, j, 1, j).wait_recv()
+                    add(sinking, j, j)
+
+                sum_copy(sinking, j, 1, count if far == 1 else j).start()
+
+        done = c - count
+
+        @pl.when(inside(done))
+        def _():
+            @pl.when(has_down)
+            def _():
+                sum_copy(done, me, 0, me).wait_recv()
+                add(done, me, me)
+
+            @pl.when(has_up)
+            def _():
+                sum_copy(done, me, 1, count).wait_recv()
+                add(done, me, count)
+
+            out_ref[done] = parts[done, :, rows(me)]
+
+        return carry
+
+    lax.fori_loop(0, planes + 2 * count - 1, step, 0)
+
+    def finish(p, carry):
+        for j in range(count):
+            @pl.when(jnp.logical_and(has_up, j <= me))
+            def _():
+                gather_copy(p, j, 0).wait_send()
+
+            @pl.when(jnp.logical_and(has_down, j >= me))
+            def _():
+                gather_copy(p, j, 1).wait_send()
+
+            @pl.when(j > me)
+            def _():
+                sum_copy(p, j, 0, j).wait_send()
+
+            @pl.when(j < me)
+            def _():
+                sum_copy(p, j, 1, j).wait_send()
+
+        return carry
+
+    lax.fori_loop(0, planes, finish, 0)
+
+
+def slab_planes(own_modes, noise_field, mode_table, turned):
+    count = lax.axis_size("my")
+    planes, _, block, mode_count = own_modes.shape
+    point_block, point_count = noise_field.shape[2:]
+    vmem = pl.BlockSpec(memory_space=pltpu.VMEM)
+    hbm = pl.BlockSpec(memory_space=pl.ANY)
+    dma = pltpu.SemaphoreType.DMA
+    flops = 8 * planes * mode_count * point_block * (point_count + mode_count)
+    return pl.pallas_call(
+        slab_kernel,
+        out_shape=jax.ShapeDtypeStruct(own_modes.shape, jnp.bfloat16),
+        in_specs=[hbm, hbm, vmem, vmem],
+        out_specs=vmem,
+        scratch_shapes=[
+            pltpu.VMEM((planes, 2, mode_count, mode_count), jnp.bfloat16),
+            pltpu.VMEM((planes, 2, mode_count, mode_count), jnp.bfloat16),
+            pltpu.VMEM((planes, count + 1, 2, block, mode_count), jnp.bfloat16),
+            pltpu.VMEM((2, 2, point_block, point_count), jnp.bfloat16),
+            dma,
+            dma((2,)),
+            dma((planes, count)),
+            dma((planes, 2, count)),
+            dma((planes, count + 1)),
+            dma((planes, 2, count)),
+        ],
+        compiler_params=pltpu.CompilerParams(
+            collective_id=0, has_side_effects=True, vmem_limit_bytes=60 * 1024 * 1024
+        ),
+        cost_estimate=pl.CostEstimate(
+            flops=flops, bytes_accessed=noise_field.size * 2, transcendentals=0
+        ),
+    )(own_modes, noise_field, mode_table, turned)
+
+
+def body(coefficients, noise_field, mode_table):
+    rep_index = lax.axis_index("rep")
+    col_index = lax.axis_index("my")
+    rep_count = lax.axis_size("rep")
+    row_count = lax.axis_size("mx")
+    col_count = lax.axis_size("my")
+    planes_dev = noise_field.shape[0]
+    planes_rep = planes_dev * row_count
+    planes_all = planes_rep * rep_count
+    mode_count = mode_table.shape[0]
+    point_count = mode_table.shape[1]
+    slab_first = point_count // 2 - planes_all // 2
+    row_block = mode_count // row_count
+    col_block = mode_count // col_count
+    point_block = point_count // col_count
+    own_block = mode_count // rep_count
+    if col_block % 16 or point_block % 128 or mode_count % 128 or col_count < 2:
+        return plain_body(coefficients, noise_field, mode_table)
+    slab_own = lax.dynamic_slice_in_dim(
+        mode_table, slab_first + rep_index * planes_rep, planes_rep, 1
+    )
+    zmodes = jnp.einsum(
+        "pabk,kz->zpba", coefficients, slab_own, preferred_element_type=jnp.float32
+    ).astype(jnp.bfloat16)
+    zmodes = zmodes.reshape(planes_rep, 2, col_block * row_block)
+    spread = lax.all_to_all(zmodes, "mx", split_axis=0, concat_axis=2, tiled=True)
+    own_modes = (
+        spread.reshape(planes_dev, 2, row_count, col_block, row_block)
+        .transpose(0, 1, 3, 2, 4)
+        .reshape(planes_dev, 2, col_block, mode_count)
+    )
+    turned = lax.dynamic_slice_in_dim(mode_table, col_index * point_block, point_block, 1).T
+    proj_rows = slab_planes(own_modes, noise_field, mode_table, turned)
+    gathered_rows = lax.all_to_all(proj_rows, "mx", split_axis=3, concat_axis=0, tiled=True)
+    slab_back = lax.dynamic_slice_in_dim(mode_table, rep_index * own_block, own_block, 0)[
+        :, slab_first : slab_first + planes_all
+    ]
+    portion = lax.all_gather(
+        gathered_rows.reshape(planes_rep, 2, col_block * row_block), "rep", axis=0, tiled=True
+    )
+    plane_grid = portion.reshape(planes_all, 2, col_block, row_block)
+    summed = jnp.einsum("zpba,nz->pabn", plane_grid, slab_back, preferred_element_type=jnp.float32)
+    return summed.astype(jnp.bfloat16)
+
 
 def solution(mesh):
     in_specs = (P(None, "mx", "my", None), P(("rep", "mx"), None, "my", None), P())

time: 986 us -> 483 us (0.49); the launches traced: 975 us -> 482 us
  blocking collectives: 277 us -> 33.8 us
  Pallas kernels: 0 us -> 229 us
  waiting for transfers between devices: 243 us -> 89.2 us
  local copies, waits for them, and re-layouts: 228 us -> 80.4 us
  other arithmetic: 99.5 us -> 0 us
  matrix products: 113 us -> 31.3 us
    all_to_all x3 -> x1, blocking collectives: 277 us -> 33.8 us  [body(): lax.all_to_all(proj_rows, 'mx', split_axis=3, concat_axis=0, tiled=True)]
    pallas_call x0 -> x1, Pallas kernels: none -> 229 us  [slab_planes(): pl.pallas_call(slab_kernel, out_shape=jax.ShapeDtypeStruct(own_modes.shap...]
    all_gather x2 -> x1, waiting for transfers between devices: 243 us -> 62.4 us  [body(): lax.all_gather(gathered_rows.reshape(planes_rep, 2, col_block * row_block...]
    dot_general x3 -> x0, matrix products: 73.4 us -> none  [the longest x1 36.1 us: body(): jnp.einsum('zpax,ay->zpxy', block_part, mode_table, preferred_element_typ...]
    all_to_all x4 -> x1, local copies, waits for them, and re-layouts: 73 us -> 6.32 us  [body(): lax.all_to_all(proj_rows, 'mx', split_axis=3, concat_axis=0, tiled=True)]
    another operation x1 -> x0, other arithmetic: 61.5 us -> none
    unnamed x4 -> x1, local copies, waits for them, and re-layouts: 50.7 us -> 0.92 us
    convert_element_type x1 -> x0, other arithmetic: 38 us -> none  [body(): noise_wide = noise_field.astype(jnp.float32)]
  transfers between devices with their start and end apart: 2 -> 2, of which waited for: 2 -> 2; matrix products, arithmetic and copies ran while one was open for 4% -> 0% of each run, Pallas kernels for 0% -> 0%
where the time goes in v1:
time: 483 us; the launch traced here: 482 us
  Pallas kernels  229 us (47%)
  waiting for transfers between devices  89.2 us (18%)
  local copies, waits for them, and re-layouts  80.4 us (17%)
  blocking collectives  33.8 us (7%)
  matrix products  31.3 us (6%)
  between operations  13.4 us (3%)
    pallas_call x1, Pallas kernels, slab_planes(): pl.pallas_call(slab_kernel, out_shape=jax.ShapeDtypeStruct(own_modes.shap...  229 us
    all_gather x1, waiting for transfers between devices, body(): lax.all_gather(gathered_rows.reshape(planes_rep, 2, col_block * row_block...  62.4 us
    all_to_all x1, blocking collectives, body(): lax.all_to_all(proj_rows, 'mx', split_axis=3, concat_axis=0, tiled=True)  33.8 us
    all_to_all x1, waiting for transfers between devices, body(): lax.all_to_all(zmodes, 'mx', split_axis=0, concat_axis=2, tiled=True)  26.8 us
    dot_general x1, matrix products, body(): jnp.einsum('pabk,kz->zpba', coefficients, slab_own, preferred_element_typ...  17.5 us
    convert_element_type x1, local copies, waits for them, and re-layouts, body(): return summed.astype(jnp.bfloat16)  13.9 us
    dot_general x1, matrix products, body(): jnp.einsum('zpba,nz->pabn', plane_grid, slab_back, preferred_element_type...  13.8 us
    all_gather x1, local copies, waits for them, and re-layouts, body(): lax.all_gather(gathered_rows.reshape(planes_rep, 2, col_block * row_block...  12.6 us
  transfers between devices with their start and end apart: 2, of which 2 were waited for; matrix products, arithmetic and copies ran while one was open for 0% of the time, Pallas kernels for 0%

profile of v1, /device:TPU:0, one launch (start us, length us, event | category | flops | bytes accessed | tf_op | source)
XLA Modules:
  0.0 481.6 jit_solution(13160060824150884766)
XLA Ops:
  6.5 17.5 %convert_bitcast_fusion.1 = bf16[32,2,96,192]{2,0,3,1:T(8,128)(2,1)S(1)} fusion(bf16[2,192,96,384]{3,2,1,0:T(8,128)(2,1)} %param.3, bf16[384,1536]{1,0:T(8,128)(2,1)} %table_ref.1, s32[]{:T(128)S(6)} %select_n.10), kind=kOutput, calls=%fused_computation.1 | convolution fusion | flops 907149312 | bytes 30769156 | tf_op jit(solution)/shard_map/pabk,kz->zpba/dot_general | solution.py:343
  24.0 3.8 copy.26
  27.8 7.9 %reshape.24 = bf16[32,2,18432]{2,1,0:T(2,128)(2,1)} reshape(bf16[32,2,96,192]{3,2,1,0:T(8,128)(2,1)} %copy.26) | data formatting | bytes 4718592 | tf_op jit(solution)/shard_map/reshape | solution.py:346
  35.7 4.3 all-to-all-start
  40.0 0.0 all-gather.2.cloned.1.call-start
  40.0 1.0 constant_dynamic-slice_fusion
  41.0 0.9 copy.29
  41.9 26.8 %all-to-all-done = bf16[32,2,18432]{2,1,0:T(2,128)(2,1)S(1)} async-done(((bf16[32,2,18432]{2,1,0:T(2,128)(2,1)}), bf16[32,2,18432]{2,1,0:T(2,128)(2,1)S(1)}, u32[]{:S(2)}, u32[]{:S(2)}) %all-to-all-start) | async-done | bytes 2359328 | tf_op jit(solution)/shard_map/all_to_all | solution.py:347
  68.7 2.1 copy.31
  70.8 4.9 %reshape.18 = bf16[16,2,2,96,192]{4,3,0,2,1:T(8,128)(2,1)S(1)} reshape(bf16[16,2,2,18432]{3,0,2,1:T(8,128)(2,1)} %bitcast.41) | data formatting | bytes 4718592 | tf_op jit(solution)/shard_map/reshape | solution.py:349
  75.7 4.9 %copy.18 = bf16[16,2,96,2,192]{4,3,2,1,0:T(2,128)(2,1)} copy(bf16[16,2,96,2,192]{4,2,0,3,1:T(8,128)(2,1)S(1)} %bitcast.38) | data formatting | bytes 4718592 | tf_op jit(solution)/shard_map/transpose | solution.py:350
  80.6 7.4 %reshape.19.own_ref = bf16[16,2,96,384]{3,2,1,0:T(8,128)(2,1)} reshape(bf16[16,2,96,2,192]{4,3,2,1,0:T(2,128)(2,1)} %copy.18) | data formatting | bytes 4718592 | tf_op jit(solution)/shard_map/reshape | solution.py:351
  88.0 229.3 %shard_map.37 = bf16[16,2,96,384]{3,2,1,0:T(8,128)(2,1)} custom-call(bf16[16,2,96,384]{3,2,1,0:T(8,128)(2,1)} %reshape.19.own_ref, bf16[16,2,384,1536]{3,2,1,0:T(8,128)(2,1)} %noise_ref.1, bf16[384,1536]{1,0:T(8,128)(2,1)} %table_ref.1, bf16[384,384]{1,0:T(8,128)(2,1)} %bitcast.42), custom_call_target="tpu_custom_call" | custom-call | flops 36238786560 | bytes 37748736 | tf_op jit(solution)/shard_map/pallas_call | solution.py:296
  317.3 8.5 %copy.20 = bf16[16,2,96,384]{2,1,0,3:T(2,128)(2,1)} copy(bf16[16,2,96,384]{3,2,1,0:T(8,128)(2,1)} %shard_map.37) | data formatting | bytes 4718592 | tf_op jit(solution)/shard_map/pallas_call | solution.py:296
  325.8 33.8 %all_to_all.30 = bf16[16,2,96,384]{2,1,0,3:T(2,128)(2,1)S(1)} all-to-all(bf16[16,2,96,384]{2,1,0,3:T(2,128)(2,1)} %copy.20), channel_id=1, replica_groups=mesh['rep'=4,'mx'=2,'my'=4] {'mx'}, dimensions={3} | all-to-all | bytes 4718592 | tf_op jit(solution)/shard_map/all_to_all | solution.py:355
  359.6 6.3 %copy.21 = bf16[16,2,96,2,192]{4,2,0,3,1:T(8,128)(2,1)} copy(bf16[16,2,96,2,192]{2,1,0,4,3:T(2,128)(2,1)S(1)} %bitcast.37) | data formatting | bytes 4718592 | tf_op jit(solution)/shard_map/all_to_all | solution.py:355
  365.9 6.2 %reshape.20 = bf16[32,2,18432]{2,0,1:T(8,128)(2,1)} reshape(bf16[2,16,2,96,192]{4,3,1,0,2:T(8,128)(2,1)} %bitcast.39) | data formatting | bytes 4718592 | tf_op jit(solution)/shard_map/reshape | solution.py:360
  372.1 0.0 all-gather.2.cloned.1.call-update
  372.1 62.4 %all-gather.2.cloned.1.call-done = bf16[128,2,18432]{2,0,1:T(8,128)(2,1)} async-done(((bf16[32,2,18432]{2,0,1:T(8,128)(2,1)}), bf16[128,2,18432]{2,0,1:T(8,128)(2,1)}) %all-gather.2.cloned.1.call-update) | async-done | bytes 9437200 | tf_op jit(solution)/shard_map/all_gather | solution.py:359
  434.5 12.6 %copy.22 = bf16[128,2,18432]{0,2,1:T(8,128)(2,1)} copy(bf16[128,2,18432]{2,0,1:T(8,128)(2,1)} %all-gather.2.cloned.1.call-done) | data formatting | bytes 18874368 | tf_op jit(solution)/shard_map/all_gather | solution.py:359
  447.1 13.8 %convert_bitcast_fusion = bf16[2,192,96,96]{1,3,2,0:T(8,128)(2,1)} fusion(bf16[128,2,96,192]{0,3,2,1:T(8,128)(2,1)} %bitcast.36, bf16[384,1536]{1,0:T(8,128)(2,1)} %table_ref.1, s32[]{:T(128)S(6)} %select_n.9, s32[]{:T(128)S(6)} %add.14), kind=kOutput, calls=%fused_computation | convolution fusion | flops 909508608 | bytes 16539656 | tf_op jit(solution)/shard_map/zpba,nz->pabn/dot_general | solution.py:363
  460.9 13.9 %copy.23 = bf16[2,192,96,96]{3,2,1,0:T(8,128)(2,1)} copy(bf16[2,192,96,96]{1,3,2,0:T(8,128)(2,1)} %convert_bitcast_fusion) | data formatting | bytes 14155776 | tf_op jit(solution)/shard_map/convert_element_type | solution.py:364
Async XLA Ops:
  35.7 33.0 %all-to-all-start = ((bf16[32,2,18432]{2,1,0:T(2,128)(2,1)}), bf16[32,2,18432]{2,1,0:T(2,128)(2,1)S(1)}, u32[]{:S(2)}, u32[]{:S(2)}) async-start(bf16[32,2,18432]{2,1,0:T(2,128)(2,1)} %reshape.24), calls=%async_computation | async-start | bytes 4718592 | tf_op jit(solution)/shard_map/all_to_all | solution.py:347
  40.0 394.6 %all-gather.2.cloned.1.call-start = ((), (), s32[]{:S(2)}) async-start(), calls=%async_computation.2 | async-start | bytes 11796480 | tf_op jit(solution)/shard_map/all_gather | solution.py:359
Sparse Core Ops, SparseCore 0:
  372.2 62.2 all-gather.1

commit v2 on v1

--- a/solution.py
+++ b/solution.py
@@ -77,11 +77,18 @@
     return summed.astype(jnp.bfloat16)
 
 def slab_kernel(own_ref, noise_ref, table_ref, turned_ref, out_ref, modes, parts, landed, noise,
-                own_sem, noise_sem, gather_recv, gather_send, sum_recv, sum_send):
+                halves, own_sem, noise_sem, gather_recv, gather_send, sum_recv, sum_send,
+                half_recv, half_send, last_recv, last_send):
     count = lax.axis_size("my")
     me = lax.axis_index("my")
-    planes = own_ref.shape[0]
+    row_count = lax.axis_size("mx")
+    row = lax.axis_index("mx")
+    rep_count = lax.axis_size("rep")
+    rep = lax.axis_index("rep")
+    planes = own_ref.shape[0] // row_count
     block = own_ref.shape[2]
+    row_block = own_ref.shape[3]
+    offsets = [(dr, dh) for dr in range(rep_count) for dh in range(row_count)]
     mode_count, point_count = table_ref.shape
     chunk = max(c for c in (512, 256, 128) if point_count % c == 0)
     up = {"my": me + 1}
@@ -99,11 +106,51 @@
     def _():
         pl.semaphore_signal(barrier, inc=1, device_id=down, device_id_type=MESH)
 
+    for dr, dh in offsets[1:]:
+        pl.semaphore_signal(
+            barrier, inc=1,
+            device_id={"rep": lax.rem(rep + dr, rep_count), "mx": lax.rem(row + dh, row_count)},
+            device_id_type=MESH,
+        )
+
     def rows(j):
         return pl.ds(pl.multiple_of(j * block, block), block)
 
     def own_copy():
-        return pltpu.make_async_copy(own_ref, modes.at[:, :, rows(me)], own_sem)
+        return pltpu.make_async_copy(
+            own_ref.at[pl.ds(row * planes, planes)], halves.at[:, row], own_sem
+        )
+
+    def half_copy(p, dh, source):
+        target = lax.rem(row + dh, row_count)
+        return pltpu.make_async_remote_copy(
+            src_ref=own_ref.at[target * planes + p],
+            dst_ref=halves.at[p, source],
+            send_sem=half_send.at[p, dh],
+            recv_sem=half_recv.at[p, dh],
+            device_id={"mx": target},
+            device_id_type=MESH,
+        )
+
+    def last_copy(p, at, received):
+        dr, dh = offsets[at]
+        target = lax.rem(row + dh, row_count)
+        if received:
+            from_rep = lax.rem(rep + rep_count - dr, rep_count)
+            from_row = lax.rem(row + row_count - dh, row_count)
+        else:
+            from_rep, from_row = rep, row
+        plane = (from_rep * row_count + from_row) * planes + p
+        if at == 0:
+            return pltpu.make_async_copy(halves.at[p, row], out_ref.at[plane], last_send.at[p, 0])
+        return pltpu.make_async_remote_copy(
+            src_ref=halves.at[p, target],
+            dst_ref=out_ref.at[plane],
+            send_sem=last_send.at[p, at],
+            recv_sem=last_recv.at[p, at],
+            device_id={"rep": lax.rem(rep + dr, rep_count), "mx": target},
+            device_id_type=MESH,
+        )
 
     def noise_copy(p):
         slot = lax.rem(p, 2)
@@ -134,8 +181,14 @@
     if planes > 1:
         noise_copy(1).start()
 
-    pl.semaphore_wait(barrier, has_up.astype(jnp.int32) + has_down.astype(jnp.int32))
-
+    pl.semaphore_wait(barrier, has_up.astype(jnp.int32) + has_down.astype(jnp.int32) + len(offsets) - 1)
+
+    def send_half(p, carry):
+        for dh in range(1, row_count):
+            half_copy(p, dh, row).start()
+        return carry
+
+    lax.fori_loop(0, planes, send_half, 0)
     own_copy().wait()
 
     def inside(p):
@@ -144,6 +197,13 @@
     def step(s, carry):
         @pl.when(s < planes)
         def _():
+            for dh in range(1, row_count):
+                half_copy(s, dh, lax.rem(row + row_count - dh, row_count)).wait_recv()
+            for part in range(2):
+                modes[s, part, rows(me)] = jnp.concatenate(
+                    [halves[s, h, part] for h in range(row_count)], 1
+                )
+
             @pl.when(has_up)
             def _():
                 gather_copy(s, me, 0).start()
@@ -256,7 +316,12 @@
                 sum_copy(done, me, 1, count).wait_recv()
                 add(done, me, count)
 
-            out_ref[done] = parts[done, :, rows(me)]
+            for part in range(2):
+                whole = parts[done, part, rows(me)]
+                for h in range(row_count):
+                    halves[done, h, part] = whole[:, h * row_block : (h + 1) * row_block]
+            for at in range(len(offsets)):
+                last_copy(done, at, False).start()
 
         return carry
 
@@ -280,6 +345,12 @@
             def _():
                 sum_copy(p, j, 1, j).wait_send()
 
+        for dh in range(1, row_count):
+            half_copy(p, dh, row).wait_send()
+        last_copy(p, 0, False).wait()
+        for at in range(1, len(offsets)):
+            last_copy(p, at, False).wait_send()
+            last_copy(p, at, True).wait_recv()
         return carry
 
     lax.fori_loop(0, planes, finish, 0)
@@ -287,7 +358,11 @@
 
 def slab_planes(own_modes, noise_field, mode_table, turned):
     count = lax.axis_size("my")
-    planes, _, block, mode_count = own_modes.shape
+    mode_count = mode_table.shape[0]
+    row_count = lax.axis_size("mx")
+    rep_count = lax.axis_size("rep")
+    planes_rep, _, block, row_block = own_modes.shape
+    planes = planes_rep // row_count
     point_block, point_count = noise_field.shape[2:]
     vmem = pl.BlockSpec(memory_space=pltpu.VMEM)
     hbm = pl.BlockSpec(memory_space=pl.ANY)
@@ -295,20 +370,25 @@
     flops = 8 * planes * mode_count * point_block * (point_count + mode_count)
     return pl.pallas_call(
         slab_kernel,
-        out_shape=jax.ShapeDtypeStruct(own_modes.shape, jnp.bfloat16),
+        out_shape=jax.ShapeDtypeStruct((planes_rep * rep_count, 2, block, row_block), jnp.bfloat16),
         in_specs=[hbm, hbm, vmem, vmem],
-        out_specs=vmem,
+        out_specs=hbm,
         scratch_shapes=[
             pltpu.VMEM((planes, 2, mode_count, mode_count), jnp.bfloat16),
             pltpu.VMEM((planes, 2, mode_count, mode_count), jnp.bfloat16),
             pltpu.VMEM((planes, count + 1, 2, block, mode_count), jnp.bfloat16),
             pltpu.VMEM((2, 2, point_block, point_count), jnp.bfloat16),
+            pltpu.VMEM((planes, row_count, 2, block, row_block), jnp.bfloat16),
             dma,
             dma((2,)),
             dma((planes, count)),
             dma((planes, 2, count)),
             dma((planes, count + 1)),
             dma((planes, 2, count)),
+            dma((planes, row_count)),
+            dma((planes, row_count)),
+            dma((planes, row_count * rep_count)),
+            dma((planes, row_count * rep_count)),
         ],
         compiler_params=pltpu.CompilerParams(
             collective_id=0, has_side_effects=True, vmem_limit_bytes=60 * 1024 * 1024
@@ -343,23 +423,11 @@
     zmodes = jnp.einsum(
         "pabk,kz->zpba", coefficients, slab_own, preferred_element_type=jnp.float32
     ).astype(jnp.bfloat16)
-    zmodes = zmodes.reshape(planes_rep, 2, col_block * row_block)
-    spread = lax.all_to_all(zmodes, "mx", split_axis=0, concat_axis=2, tiled=True)
-    own_modes = (
-        spread.reshape(planes_dev, 2, row_count, col_block, row_block)
-        .transpose(0, 1, 3, 2, 4)
-        .reshape(planes_dev, 2, col_block, mode_count)
-    )
     turned = lax.dynamic_slice_in_dim(mode_table, col_index * point_block, point_block, 1).T
-    proj_rows = slab_planes(own_modes, noise_field, mode_table, turned)
-    gathered_rows = lax.all_to_all(proj_rows, "mx", split_axis=3, concat_axis=0, tiled=True)
+    plane_grid = slab_planes(zmodes, noise_field, mode_table, turned)
     slab_back = lax.dynamic_slice_in_dim(mode_table, rep_index * own_block, own_block, 0)[
         :, slab_first : slab_first + planes_all
     ]
-    portion = lax.all_gather(
-        gathered_rows.reshape(planes_rep, 2, col_block * row_block), "rep", axis=0, tiled=True
-    )
-    plane_grid = portion.reshape(planes_all, 2, col_block, row_block)
     summed = jnp.einsum("zpba,nz->pabn", plane_grid, slab_back, preferred_element_type=jnp.float32)
     return summed.astype(jnp.bfloat16)
 

time: 483 us -> 315 us (0.65)
  waiting for transfers between devices: 89.2 us -> 0 us
  local copies, waits for them, and re-layouts: 80.4 us -> 19.5 us
  blocking collectives: 33.8 us -> 0 us
  Pallas kernels: 229 us -> 256 us
  between operations: 13.4 us -> 0.02 us
    all_gather x1 -> x0, waiting for transfers between devices: 62.4 us -> none  [body(): lax.all_gather(gathered_rows.reshape(planes_rep, 2, col_block * row_block...]
    all_to_all x1 -> x0, blocking collectives: 33.8 us -> none  [body(): lax.all_to_all(proj_rows, 'mx', split_axis=3, concat_axis=0, tiled=True)]
    reshape x5 -> x0, local copies, waits for them, and re-layouts: 30.2 us -> none  [the longest x2 11.7 us: body(): zmodes = zmodes.reshape(planes_rep, 2, col_block * row_block)]
    all_to_all x1 -> x0, waiting for transfers between devices: 26.8 us -> none  [body(): lax.all_to_all(zmodes, 'mx', split_axis=0, concat_axis=2, tiled=True)]
    pallas_call x1, Pallas kernels: 229 us -> 256 us  [slab_planes(): pl.pallas_call(slab_kernel, out_shape=jax.ShapeDtypeStruct((planes_rep *...]
    all_gather x1 -> x0, local copies, waits for them, and re-layouts: 12.6 us -> none  [body(): lax.all_gather(gathered_rows.reshape(planes_rep, 2, col_block * row_block...]
    pallas_call x1 -> x0, local copies, waits for them, and re-layouts: 8.53 us -> none  [slab_planes(): pl.pallas_call(slab_kernel, out_shape=jax.ShapeDtypeStruct(own_modes.shap...]
    all_to_all x2 -> x0, local copies, waits for them, and re-layouts: 8.41 us -> none  [the longest x1 6.32 us: body(): lax.all_to_all(proj_rows, 'mx', split_axis=3, concat_axis=0, tiled=True)]
  transfers between devices with their start and end apart: 2 -> 0, of which waited for: 2 -> 0; matrix products, arithmetic and copies ran while one was open for 0% -> 0% of each run, Pallas kernels for 0% -> 0%
where the time goes in v2:
time: 315 us; the launch traced here: 310 us
  Pallas kernels  256 us (81%)
  matrix products  34.3 us (11%)
  local copies, waits for them, and re-layouts  19.5 us (6%)
    pallas_call x1, Pallas kernels, slab_planes(): pl.pallas_call(slab_kernel, out_shape=jax.ShapeDtypeStruct((planes_rep *...  256 us
    dot_general x1, matrix products, body(): jnp.einsum('pabk,kz->zpba', coefficients, slab_own, preferred_element_typ...  17.5 us
    dot_general x1, matrix products, body(): jnp.einsum('zpba,nz->pabn', plane_grid, slab_back, preferred_element_type...  16.8 us
    convert_element_type x1, local copies, waits for them, and re-layouts, body(): return summed.astype(jnp.bfloat16)  13.9 us

profile of v2, /device:TPU:0, one launch (start us, length us, event | category | flops | bytes accessed | tf_op | source)
XLA Modules:
  0.0 309.9 jit_solution(4517143358514703293)
XLA Ops:
  0.0 1.0 constant_dynamic-slice_fusion
  1.0 0.9 copy.10
  1.9 17.5 %fusion.4 = bf16[32,2,192,96]{3,0,2,1:T(8,128)(2,1)S(1)} fusion(bf16[2,192,96,384]{3,2,1,0:T(8,128)(2,1)} %param.3, bf16[384,1536]{1,0:T(8,128)(2,1)} %table_ref.1, s32[]{:T(128)S(6)} %select_n.10), kind=kOutput, calls=%fused_computation.4 | convolution fusion | flops 905969664 | bytes 30769156 | tf_op jit(solution)/shard_map/pabk,kz->zpba/dot_general | solution.py:423
  19.4 3.8 %copy.8 = bf16[32,2,192,96]{2,3,1,0:T(8,128)(2,1)} copy(bf16[32,2,192,96]{3,0,2,1:T(8,128)(2,1)S(1)} %fusion.4) | data formatting | bytes 4718592 | tf_op jit(solution)/shard_map/pabk,kz->zpba/dot_general | solution.py:423
  23.2 256.0 %shard_map.37 = bf16[128,2,96,192]{3,2,1,0:T(8,128)(2,1)} custom-call(bf16[32,2,96,192]{3,2,1,0:T(8,128)(2,1)} %bitcast.17, bf16[16,2,384,1536]{3,2,1,0:T(8,128)(2,1)} %noise_ref.1, bf16[384,1536]{1,0:T(8,128)(2,1)} %table_ref.1, bf16[384,384]{1,0:T(8,128)(2,1)} %bitcast.18), custom_call_target="tpu_custom_call" | custom-call | flops 36238786560 | bytes 37748736 | tf_op jit(solution)/shard_map/pallas_call | solution.py:371
  279.2 16.8 %convert_bitcast_fusion = bf16[2,192,96,96]{1,3,2,0:T(8,128)(2,1)} fusion(bf16[128,2,96,192]{3,2,1,0:T(8,128)(2,1)} %shard_map.37, bf16[384,1536]{1,0:T(8,128)(2,1)} %table_ref.1, s32[]{:T(128)S(6)} %select_n.9, s32[]{:T(128)S(6)} %add.14), kind=kOutput, calls=%fused_computation.2 | convolution fusion | flops 909508608 | bytes 19685384 | tf_op jit(solution)/shard_map/zpba,nz->pabn/dot_general | solution.py:431
  296.0 13.9 %copy.6 = bf16[2,192,96,96]{3,2,1,0:T(8,128)(2,1)} copy(bf16[2,192,96,96]{1,3,2,0:T(8,128)(2,1)} %convert_bitcast_fusion) | data formatting | bytes 14155776 | tf_op jit(solution)/shard_map/convert_element_type | solution.py:432

commit v3 on v2

--- a/solution.py
+++ b/solution.py
@@ -302,7 +302,7 @@
 
                 sum_copy(sinking, j, 1, count if far == 1 else j).start()
 
-        done = c - count
+        done = c - (count - 1)
 
         @pl.when(inside(done))
         def _():
@@ -325,7 +325,7 @@
 
         return carry
 
-    lax.fori_loop(0, planes + 2 * count - 1, step, 0)
+    lax.fori_loop(0, planes + 2 * count - 2, step, 0)
 
     def finish(p, carry):
         for j in range(count):

time: 315 us -> 307 us (0.975)
  Pallas kernels: 256 us -> 248 us
    pallas_call x1, Pallas kernels: 256 us -> 248 us  [slab_planes(): pl.pallas_call(slab_kernel, out_shape=jax.ShapeDtypeStruct((planes_rep *...]
where the time goes in v3:
time: 307 us; the launch traced here: 302 us
  Pallas kernels  248 us (81%)
  matrix products  34.3 us (11%)
  local copies, waits for them, and re-layouts  19.5 us (6%)
    pallas_call x1, Pallas kernels, slab_planes(): pl.pallas_call(slab_kernel, out_shape=jax.ShapeDtypeStruct((planes_rep *...  248 us
    dot_general x1, matrix products, body(): jnp.einsum('pabk,kz->zpba', coefficients, slab_own, preferred_element_typ...  17.5 us
    dot_general x1, matrix products, body(): jnp.einsum('zpba,nz->pabn', plane_grid, slab_back, preferred_element_type...  16.8 us
    convert_element_type x1, local copies, waits for them, and re-layouts, body(): return summed.astype(jnp.bfloat16)  13.9 us

profile of v3, /device:TPU:0, one launch (start us, length us, event | category | flops | bytes accessed | tf_op | source)
XLA Modules:
  0.0 302.0 jit_solution(17672028078717098582)
XLA Ops:
  0.0 1.0 constant_dynamic-slice_fusion
  1.0 0.9 copy.10
  1.9 17.5 %fusion.4 = bf16[32,2,192,96]{3,0,2,1:T(8,128)(2,1)S(1)} fusion(bf16[2,192,96,384]{3,2,1,0:T(8,128)(2,1)} %param.3, bf16[384,1536]{1,0:T(8,128)(2,1)} %table_ref.1, s32[]{:T(128)S(6)} %select_n.10), kind=kOutput, calls=%fused_computation.4 | convolution fusion | flops 905969664 | bytes 30769156 | tf_op jit(solution)/shard_map/pabk,kz->zpba/dot_general | solution.py:423
  19.4 3.8 %copy.8 = bf16[32,2,192,96]{2,3,1,0:T(8,128)(2,1)} copy(bf16[32,2,192,96]{3,0,2,1:T(8,128)(2,1)S(1)} %fusion.4) | data formatting | bytes 4718592 | tf_op jit(solution)/shard_map/pabk,kz->zpba/dot_general | solution.py:423
  23.2 248.2 %shard_map.37 = bf16[128,2,96,192]{3,2,1,0:T(8,128)(2,1)} custom-call(bf16[32,2,96,192]{3,2,1,0:T(8,128)(2,1)} %bitcast.17, bf16[16,2,384,1536]{3,2,1,0:T(8,128)(2,1)} %noise_ref.1, bf16[384,1536]{1,0:T(8,128)(2,1)} %table_ref.1, bf16[384,384]{1,0:T(8,128)(2,1)} %bitcast.18), custom_call_target="tpu_custom_call" | custom-call | flops 36238786560 | bytes 37748736 | tf_op jit(solution)/shard_map/pallas_call | solution.py:371
  271.4 16.8 %convert_bitcast_fusion = bf16[2,192,96,96]{1,3,2,0:T(8,128)(2,1)} fusion(bf16[128,2,96,192]{3,2,1,0:T(8,128)(2,1)} %shard_map.37, bf16[384,1536]{1,0:T(8,128)(2,1)} %table_ref.1, s32[]{:T(128)S(6)} %select_n.9, s32[]{:T(128)S(6)} %add.14), kind=kOutput, calls=%fused_computation.2 | convolution fusion | flops 909508608 | bytes 19685384 | tf_op jit(solution)/shard_map/zpba,nz->pabn/dot_general | solution.py:431
  288.2 13.9 %copy.6 = bf16[2,192,96,96]{3,2,1,0:T(8,128)(2,1)} copy(bf16[2,192,96,96]{1,3,2,0:T(8,128)(2,1)} %convert_bitcast_fusion) | data formatting | bytes 14155776 | tf_op jit(solution)/shard_map/convert_element_type | solution.py:432
